TPU v7x, 32 devices: a whole 2x2x4 slice. The times are simulated.
32 devices in a mesh: freq: 32 (over z, y, x, core).
Axes of the slice: x: 2, y: 2, z: 4, core: 2. Of those that a mesh axis runs over, the one named last changes fastest.
Arguments:
- pulses: float32 [1, 2, 30, 65536], P(None, None, None, 'freq'), may hold values from -4 to 4
- coupling: float32 [2, 30, 30, 65536], P(None, None, None, 'freq'), may hold values from -0.4 to 0.4
- dispersion_terms: float32 [3, 30], replicated, may hold values from -3 to 3
- kerr_gain: float32 [30], replicated, may hold values from 0.01 to 0.08
Outputs:
- evolved: float32 [1, 2, 30, 65536], P(None, None, None, 'freq')
All inputs are finite; a program needn't handle non-finite values.
Results may differ from a plain program's by a relative error of at most 0.00027.
Values sent between devices are 32-bit elements; how exact they have to be, the bound alone decides.
A program may use at most 128 MiB of HBM per device.

v0:
```python
import jax
import jax.numpy as jnp
from jax import lax
from jax.sharding import PartitionSpec as P

STEPS = 2
HIGHEST = lax.Precision.HIGHEST


def angle_table(first, second, modulus, orient):
    turns = first[:, None] * second[None, :] % modulus
    radians = turns.astype(jnp.float32) * (2.0 * jnp.pi / modulus)
    return (jnp.cos(radians), orient * jnp.sin(radians))


def rotate(real_part, imag_part, cosine, sine):
    return (real_part * cosine - imag_part * sine, real_part * sine + imag_part * cosine)


def transform(stacked, cosine, sine):
    real_part = stacked[:, 0]
    imag_part = stacked[:, 1]
    out_real = jnp.matmul(real_part, cosine, precision=HIGHEST) - jnp.matmul(
        imag_part, sine, precision=HIGHEST
    )
    out_imag = jnp.matmul(real_part, sine, precision=HIGHEST) + jnp.matmul(
        imag_part, cosine, precision=HIGHEST
    )
    return jnp.stack((out_real, out_imag), axis=1)


def nonlinear_phase(stacked, kerr_gain):
    magnitude = stacked[:, 0] ** 2 + stacked[:, 1] ** 2
    total_power = jnp.sum(magnitude, axis=1, keepdims=True)
    gains = kerr_gain.reshape((1, -1) + (1,) * (magnitude.ndim - 2))
    angles = gains * (2.0 * total_power - magnitude)
    real_part, imag_part = rotate(stacked[:, 0], stacked[:, 1], jnp.cos(angles), jnp.sin(angles))
    return jnp.stack((real_part, imag_part), axis=1)


def per_device(pulses, coupling, dispersion_terms, kerr_gain):
    shards = lax.axis_size("freq")
    device = lax.axis_index("freq")
    mode_count = pulses.shape[2]
    local_count = pulses.shape[3]
    groups = local_count // shards
    total_count = local_count * shards
    column_index = jnp.arange(shards, dtype=jnp.int32)
    row_index = jnp.arange(local_count, dtype=jnp.int32)
    short_cos, short_sin = angle_table(column_index, column_index, shards, -1.0)
    inverse_short_cos, inverse_short_sin = angle_table(column_index, column_index, shards, 1.0)
    long_cos, long_sin = angle_table(row_index, row_index, local_count, -1.0)
    inverse_long_cos, inverse_long_sin = angle_table(row_index, row_index, local_count, 1.0)
    sample_rows = jnp.arange(groups, dtype=jnp.int32) * shards + device
    twist_cos, twist_sin = angle_table(sample_rows, column_index, total_count, -1.0)
    untwist_cos, untwist_sin = angle_table(row_index, jnp.reshape(device, (1,)), total_count, 1.0)
    untwist_cos = untwist_cos.reshape(-1)
    untwist_sin = untwist_sin.reshape(-1)
    bins = device + shards * row_index
    signed_bin = jnp.where(bins < total_count // 2, bins, bins - total_count).astype(jnp.float32)
    angular = signed_bin / (total_count // 2)
    dispersion = (
        dispersion_terms[0][:, None] * angular
        + dispersion_terms[1][:, None] * angular**2 / 2
        + dispersion_terms[2][:, None] * angular**3 / 6
    )
    spread_cos = jnp.cos(dispersion)
    spread_sin = jnp.sin(dispersion)
    identity = jnp.eye(mode_count, dtype=jnp.float32)[:, :, None]
    mixing_real = coupling[0] + identity
    mixing_imag = coupling[1]
    blocks = pulses.reshape(pulses.shape[0], 2, mode_count, groups, shards)
    columns = lax.all_to_all(blocks, "freq", split_axis=4, concat_axis=4, tiled=True)
    for repeat in range(STEPS):
        spectral = transform(columns, short_cos, short_sin)
        forward_real_part, forward_imag_part = rotate(
            spectral[:, 0], spectral[:, 1], twist_cos, twist_sin
        )
        evolve_rows = lax.all_to_all(
            jnp.stack((forward_real_part, forward_imag_part), axis=1),
            "freq",
            split_axis=4,
            concat_axis=4,
            tiled=True,
        )
        flat = evolve_rows.reshape(evolve_rows.shape[0], 2, mode_count, local_count)
        spectrum = transform(flat, long_cos, long_sin)
        spec_real = spectrum[:, 0]
        spec_imag = spectrum[:, 1]
        mixed_real = jnp.einsum(
            "nmk,bmk->bnk", mixing_real, spec_real, precision=HIGHEST
        ) - jnp.einsum("nmk,bmk->bnk", mixing_imag, spec_imag, precision=HIGHEST)
        mixed_imag = jnp.einsum(
            "nmk,bmk->bnk", mixing_real, spec_imag, precision=HIGHEST
        ) + jnp.einsum("nmk,bmk->bnk", mixing_imag, spec_real, precision=HIGHEST)
        real_part, imag_part = rotate(mixed_real, mixed_imag, spread_cos, spread_sin)
        inverted = transform(
            jnp.stack((real_part, imag_part), axis=1), inverse_long_cos, inverse_long_sin
        )
        real_part, imag_part = rotate(inverted[:, 0], inverted[:, 1], untwist_cos, untwist_sin)
        moved = jnp.stack((real_part, imag_part), axis=1).reshape(evolve_rows.shape)
        columns = nonlinear_phase(
            transform(
                lax.all_to_all(moved, "freq", split_axis=4, concat_axis=4, tiled=True),
                inverse_short_cos,
                inverse_short_sin,
            )
            * (1.0 / total_count),
            kerr_gain,
        )
    returned = lax.all_to_all(columns, "freq", split_axis=4, concat_axis=4, tiled=True)
    return returned.reshape(columns.shape[0], 2, mode_count, local_count)


def solution(mesh):
    in_specs = (P(None, None, None, "freq"), P(None, None, None, "freq"), P(), P())
    out_specs = P(None, None, None, "freq")
    return jax.shard_map(
        per_device, mesh=mesh, in_specs=in_specs, out_specs=out_specs, check_vma=False
    )
```

profile of v0, /device:TPU:0, one launch (start us, length us, event | category | flops | bytes accessed | tf_op | source)
XLA Modules:
  0.0 1394.7 jit_solution(16185330490249208704)
XLA Ops:
  0.0 1.9 reshape.856
  2.8 1.8 reshape.893
  4.6 7.3 all-to-all-start
  12.1 14.9 %all-to-all-done = f32[32,1,3840]{2,1,0:T(1,128)S(1)} async-done(((f32[32,1,3840]{2,1,0:T(1,128)}), f32[32,1,3840]{2,1,0:T(1,128)S(1)}, u32[]{:S(2)}, u32[]{:S(2)}) %all-to-all-start) | async-done | bytes 491552 | tf_op jit(solution)/shard_map/all_to_all | solution.py:73
  27.6 1.8 reduce.20
  34.3 1.8 reshape.895
  36.1 3.1 all-to-all-start.1
  39.2 19.7 %fusion.344 = (f32[1,30,30,2048]{3,0,2,1:T(1,128)}, f32[1,30,30,2048]{3,0,2,1:T(1,128)}) fusion(f32[2,30,30,2048]{3,0,2,1:T(2,128)} %param.5), kind=kLoop, calls=%fused_computation.366 | loop fusion | bytes 29491200 | tf_op jit(solution)/shard_map/slice | solution.py:70
  60.3 1.8 reduce.21
  65.1 71.2 %fusion.12 = f32[30,2048]{1,0:T(8,128)S(1)} fusion(f32[1,1,30,2048]{3,1,2,0:T(1,128)S(1)} %get-tuple-element.41), kind=kOutput, calls=%fused_computation.15 | convolution fusion | flops 1572864000 | bytes 491520 | tf_op jit(solution)/shard_map/dot_general | solution.py:23
  136.3 71.4 %fusion.10 = f32[30,2048]{1,0:T(8,128)S(1)} fusion(f32[1,1,30,2048]{3,1,2,0:T(1,128)S(1)} %get-tuple-element.42), kind=kOutput, calls=%fused_computation.13 | convolution fusion | flops 1572864000 | bytes 491520 | tf_op jit(solution)/shard_map/dot_general | solution.py:26
  207.7 70.6 %fusion.65 = f32[2048,30]{0,1:T(8,128)S(1)} fusion(f32[30,2048]{1,0:T(8,128)S(1)} %fusion.12, f32[1,1,30,2048]{3,1,2,0:T(1,128)S(1)} %get-tuple-element.42), kind=kOutput, calls=%fused_computation.52 | convolution fusion | flops 1568731136 | bytes 737280 | tf_op jit(solution)/shard_map/dot_general | solution.py:23
  278.4 70.4 %fusion.71 = f32[2048,30]{0,1:T(8,128)S(1)} fusion(f32[30,2048]{1,0:T(8,128)S(1)} %fusion.10, f32[1,1,30,2048]{3,1,2,0:T(1,128)S(1)} %get-tuple-element.41), kind=kOutput, calls=%fused_computation.54 | convolution fusion | flops 1568731136 | bytes 737280 | tf_op jit(solution)/shard_map/dot_general | solution.py:26
  348.8 11.7 multiply_reduce_fusion.6
  361.2 1.3 copy.73
  362.5 1.4 copy.80
  364.0 6.9 fusion.100
  370.8 74.2 %fusion.30 = f32[30,2048]{1,0:T(8,128)S(1)} fusion(f32[30,2048]{0,1:T(8,128)S(1)} %get-tuple-element.21), kind=kOutput, calls=%fused_computation.28 | convolution fusion | flops 1568669696 | bytes 491520 | tf_op jit(solution)/shard_map/dot_general | solution.py:23
  445.1 74.4 %fusion.28 = f32[30,2048]{1,0:T(8,128)S(1)} fusion(f32[1,30,2048]{1,2,0:T(8,128)S(1)} %get-tuple-element.22), kind=kOutput, calls=%fused_computation.27 | convolution fusion | flops 1568669696 | bytes 491520 | tf_op jit(solution)/shard_map/dot_general | solution.py:26
  519.5 74.7 %fusion.50 = f32[30,2048]{1,0:T(8,128)S(1)} fusion(f32[30,2048]{1,0:T(8,128)S(1)} %fusion.30, f32[1,30,2048]{1,2,0:T(8,128)S(1)} %get-tuple-element.22), kind=kOutput, calls=%fused_computation.47 | convolution fusion | flops 1568731136 | bytes 737280 | tf_op jit(solution)/shard_map/dot_general | solution.py:23
  594.3 75.0 %multiply_subtract_fusion.2 = (f32[30,2048]{1,0:T(8,128)S(1)}, f32[30,2048]{1,0:T(8,128)S(1)}) fusion(f32[30,2048]{1,0:T(8,128)S(1)} %fusion.50, f32[2048]{0:T(1024)S(1)} %copy-done.12, f32[2048]{0:T(1024)S(1)} %copy-done.14, f32[30,2048]{1,0:T(8,128)S(1)} %fusion.28, f32[30,2048]{0,1:T(8,128)S(1)} %get-tuple-element.21), kind=kOutput, calls=%fused_computation.146 | convolution fusion | flops 1569099776 | bytes 1245184 | tf_op jit(solution)/shard_map/dot_general | solution.py:26
  670.9 1.4 pad_maximum_fusion
  674.3 20.9 %all_to_all.30 = f32[32,1,3840]{2,1,0:T(1,128)S(1)} all-to-all(f32[32,1,3840]{2,1,0:T(1,128)S(1)} %reshape.897), channel_id=1, replica_groups=mesh['freq'=32] {'freq'}, dimensions={0} | all-to-all | bytes 983040 | tf_op jit(solution)/shard_map/all_to_all | solution.py:104
  695.2 1.8 reduce.22
  701.3 2.1 fusion.107
  704.7 2.5 convolution_add_fusion.1
  707.3 2.6 subtract_bitcast_fusion
  711.8 17.7 %all_to_all.31 = f32[32,1,3840]{2,1,0:T(1,128)S(1)} all-to-all(f32[32,1,3840]{2,1,0:T(1,128)S(1)} %reshape.899), channel_id=1, replica_groups=mesh['freq'=32] {'freq'}, dimensions={0} | all-to-all | bytes 983040 | tf_op jit(solution)/shard_map/all_to_all | solution.py:79
  729.4 1.8 reduce.23
  734.2 71.6 %fusion.8 = f32[30,2048]{1,0:T(8,128)S(1)} fusion(f32[1,1,30,2048]{3,1,2,0:T(1,128)S(1)} %get-tuple-element.39), kind=kOutput, calls=%fused_computation.11 | convolution fusion | flops 1572864000 | bytes 491520 | tf_op jit(solution)/shard_map/dot_general | solution.py:23
  805.9 71.4 %fusion.6 = f32[30,2048]{1,0:T(8,128)S(1)} fusion(f32[1,1,30,2048]{3,1,2,0:T(1,128)S(1)} %get-tuple-element.40), kind=kOutput, calls=%fused_computation.9 | convolution fusion | flops 1572864000 | bytes 491520 | tf_op jit(solution)/shard_map/dot_general | solution.py:26
  877.3 70.4 %fusion.77 = f32[2048,30]{0,1:T(8,128)S(1)} fusion(f32[30,2048]{1,0:T(8,128)S(1)} %fusion.8, f32[1,1,30,2048]{3,1,2,0:T(1,128)S(1)} %get-tuple-element.40), kind=kOutput, calls=%fused_computation.56 | convolution fusion | flops 1568731136 | bytes 737280 | tf_op jit(solution)/shard_map/dot_general | solution.py:23
  947.7 70.6 %fusion.83 = f32[2048,30]{0,1:T(8,128)S(1)} fusion(f32[30,2048]{1,0:T(8,128)S(1)} %fusion.6, f32[1,1,30,2048]{3,1,2,0:T(1,128)S(1)} %get-tuple-element.39), kind=kOutput, calls=%fused_computation.58 | convolution fusion | flops 1568731136 | bytes 737280 | tf_op jit(solution)/shard_map/dot_general | solution.py:26
  1018.4 11.7 multiply_reduce_fusion.2
  1030.8 1.3 copy.87
  1032.1 1.3 copy.94
  1033.5 6.9 fusion.95
  1040.4 74.2 %fusion.22 = f32[30,2048]{1,0:T(8,128)S(1)} fusion(f32[30,2048]{0,1:T(8,128)S(1)} %get-tuple-element.19), kind=kOutput, calls=%fused_computation.24 | convolution fusion | flops 1568669696 | bytes 491520 | tf_op jit(solution)/shard_map/dot_general | solution.py:23
  1114.6 74.2 %fusion.20 = f32[30,2048]{1,0:T(8,128)S(1)} fusion(f32[1,30,2048]{1,2,0:T(8,128)S(1)} %get-tuple-element.20), kind=kOutput, calls=%fused_computation.23 | convolution fusion | flops 1568669696 | bytes 491520 | tf_op jit(solution)/shard_map/dot_general | solution.py:26
  1188.9 75.0 %fusion.56 = f32[30,2048]{1,0:T(8,128)S(1)} fusion(f32[30,2048]{1,0:T(8,128)S(1)} %fusion.22, f32[1,30,2048]{1,2,0:T(8,128)S(1)} %get-tuple-element.20), kind=kOutput, calls=%fused_computation.49 | convolution fusion | flops 1568731136 | bytes 737280 | tf_op jit(solution)/shard_map/dot_general | solution.py:23
  1263.9 74.8 %multiply_subtract_fusion.1 = (f32[30,2048]{1,0:T(8,128)S(1)}, f32[30,2048]{1,0:T(8,128)S(1)}) fusion(f32[30,2048]{1,0:T(8,128)S(1)} %fusion.56, f32[2048]{0:T(1024)S(1)} %copy-done.13, f32[2048]{0:T(1024)S(1)} %copy-done.15, f32[30,2048]{1,0:T(8,128)S(1)} %fusion.20, f32[30,2048]{0,1:T(8,128)S(1)} %get-tuple-element.19), kind=kOutput, calls=%fused_computation.144 | convolution fusion | flops 1569099776 | bytes 1245184 | tf_op jit(solution)/shard_map/dot_general | solution.py:26
  1340.2 1.4 pad_maximum_fusion.1
  1343.6 17.9 %all_to_all.32 = f32[32,1,3840]{2,1,0:T(1,128)S(1)} all-to-all(f32[32,1,3840]{2,1,0:T(1,128)S(1)} %reshape.901), channel_id=1, replica_groups=mesh['freq'=32] {'freq'}, dimensions={0} | all-to-all | bytes 983040 | tf_op jit(solution)/shard_map/all_to_all | solution.py:104
  1361.5 1.8 reduce.24
  1367.6 2.1 multiply_subtract_fusion
  1371.6 17.7 %all_to_all.33 = f32[32,1,3840]{2,1,0:T(1,128)S(1)} all-to-all(f32[32,1,3840]{2,1,0:T(1,128)S(1)} %reshape.903), channel_id=1, replica_groups=mesh['freq'=32] {'freq'}, dimensions={0} | all-to-all | bytes 983040 | tf_op jit(solution)/shard_map/all_to_all | solution.py:111
  1389.3 1.8 reduce.25
  1392.7 1.8 reshape.873
  (136 shorter events, 37.0 us)
Async XLA Ops:
  4.6 22.4 %all-to-all-start = ((f32[32,1,3840]{2,1,0:T(1,128)}), f32[32,1,3840]{2,1,0:T(1,128)S(1)}, u32[]{:S(2)}, u32[]{:S(2)}) async-start(f32[32,1,3840]{2,1,0:T(1,128)} %reshape.893), calls=%async_computation | async-start | bytes 983040 | tf_op jit(solution)/shard_map/all_to_all | solution.py:73
  12.1 46.8 %copy-start = (f32[64,32]{0,1:T(8,128)}, f32[64,32]{0,1:T(8,128)S(1)}, u32[]{:S(2)}) copy-start(f32[64,32]{0,1:T(8,128)S(1)} %get-tuple-element.46) | copy-start | bytes 24580
  12.1 46.8 %copy-start.2 = (f32[64,32]{0,1:T(8,128)}, f32[64,32]{0,1:T(8,128)S(1)}, u32[]{:S(2)}) copy-start(f32[64,32]{0,1:T(8,128)S(1)} %get-tuple-element.47) | copy-start | bytes 24580
  36.1 24.2 %all-to-all-start.1 = ((f32[32,1,3840]{2,1,0:T(1,128)}), f32[32,1,3840]{2,1,0:T(1,128)S(1)}, u32[]{:S(2)}, u32[]{:S(2)}) async-start(f32[32,1,3840]{2,1,0:T(1,128)} %reshape.895), calls=%async_computation.1 | async-start | bytes 983040 | tf_op jit(solution)/shard_map/all_to_all | solution.py:79
  39.2 21.0 %copy-start.24 = (f32[3,30]{1,0:T(4,128)S(1)}, f32[3,30]{1,0:T(4,128)}, u32[]{:S(2)}) copy-start(f32[3,30]{1,0:T(4,128)} %param.6) | copy-start | bytes 1084
  58.9 305.0 %copy-start.6 = (f32[2048]{0:T(1024)}, f32[2048]{0:T(1024)S(1)}, u32[]{:S(2)}) copy-start(f32[2048]{0:T(1024)S(1)} %fusion.202) | copy-start | bytes 24580
  58.9 289.8 %copy-start.4 = (f32[30,30]{1,0:T(8,128)}, f32[30,30]{1,0:T(8,128)S(1)}, u32[]{:S(2)}) copy-start(f32[30,30]{1,0:T(8,128)S(1)} %fusion.163) | copy-start | bytes 10804
  59.6 304.3 %copy-start.8 = (f32[2048]{0:T(1024)}, f32[2048]{0:T(1024)S(1)}, u32[]{:S(2)}) copy-start(f32[2048]{0:T(1024)S(1)} %get-tuple-element.48) | copy-start | bytes 24580
  60.3 303.7 %copy-start.10 = (f32[2048]{0:T(1024)}, f32[2048]{0:T(1024)S(1)}, u32[]{:S(2)}) copy-start(f32[2048]{0:T(1024)S(1)} %get-tuple-element.51) | copy-start | bytes 24580
  60.3 303.7 %copy-start.16 = (f32[30]{0:T(128)}, f32[30]{0:T(128)S(1)}, u32[]{:S(2)}) copy-start(f32[30]{0:T(128)S(1)} %get-tuple-element.43) | copy-start | bytes 364
  60.3 303.6 %copy-start.18 = (f32[30]{0:T(128)}, f32[30]{0:T(128)S(1)}, u32[]{:S(2)}) copy-start(f32[30]{0:T(128)S(1)} %get-tuple-element.44) | copy-start | bytes 364
  60.3 303.6 %copy-start.20 = (f32[30]{0:T(128)}, f32[30]{0:T(128)S(1)}, u32[]{:S(2)}) copy-start(f32[30]{0:T(128)S(1)} %get-tuple-element.45) | copy-start | bytes 364
  207.7 141.0 %slice-start = ((s8[7372800]{0:T(1024)(128)(4,1)}), s8[4194304]{0:T(1024)(128)(4,1)S(1)}, s32[]{:S(2)}) async-start(s8[7372800]{0:T(1024)(128)(4,1)} %bitcast.327), calls=%async_computation.6 | async-start | bytes 8388608
  207.7 141.0 %slice-start.4 = ((s8[7372800]{0:T(1024)(128)(4,1)}), s8[4194304]{0:T(1024)(128)(4,1)S(1)}, s32[]{:S(2)}) async-start(s8[7372800]{0:T(1024)(128)(4,1)} %bitcast.331), calls=%async_computation.10 | async-start | bytes 8388608
  278.3 70.4 %slice-start.1 = ((s8[7372800]{0:T(1024)(128)(4,1)}), s8[3178496]{0:T(1024)(128)(4,1)S(1)}, s32[]{:S(2)}) async-start(s8[7372800]{0:T(1024)(128)(4,1)} %bitcast.327), calls=%async_computation.7 | async-start | bytes 6356992
  278.4 70.4 %slice-start.5 = ((s8[7372800]{0:T(1024)(128)(4,1)}), s8[3178496]{0:T(1024)(128)(4,1)S(1)}, s32[]{:S(2)}) async-start(s8[7372800]{0:T(1024)(128)(4,1)} %bitcast.331), calls=%async_computation.11 | async-start | bytes 6356992
  519.5 74.8 %copy-start.12 = (f32[2048]{0:T(1024)S(1)}, f32[2048]{0:T(1024)}, u32[]{:S(2)}) copy-start(f32[2048]{0:T(1024)} %get-tuple-element.49) | copy-start | bytes 24580
  519.5 74.8 %copy-start.14 = (f32[2048]{0:T(1024)S(1)}, f32[2048]{0:T(1024)}, u32[]{:S(2)}) copy-start(f32[2048]{0:T(1024)} %get-tuple-element.50) | copy-start | bytes 24580
  669.3 32.0 %copy-start.22 = (f32[30]{0:T(128)S(1)}, f32[30]{0:T(128)}, u32[]{:S(2)}) copy-start(f32[30]{0:T(128)} %param.7) | copy-start | bytes 364
  669.3 37.9 %copy-start.1 = (f32[64,32]{0,1:T(8,128)S(1)}, f32[64,32]{0,1:T(8,128)}, u32[]{:S(2)}) copy-start(f32[64,32]{0,1:T(8,128)} %copy-done) | copy-start | bytes 24580
  669.3 37.9 %copy-start.3 = (f32[64,32]{0,1:T(8,128)S(1)}, f32[64,32]{0,1:T(8,128)}, u32[]{:S(2)}) copy-start(f32[64,32]{0,1:T(8,128)} %copy-done.2) | copy-start | bytes 24580
  805.8 212.4 %slice-start.2 = ((s8[7372800]{0:T(1024)(128)(4,1)}), s8[4194304]{0:T(1024)(128)(4,1)S(1)}, s32[]{:S(2)}) async-start(s8[7372800]{0:T(1024)(128)(4,1)} %bitcast.329), calls=%async_computation.8 | async-start | bytes 8388608
  805.8 212.4 %slice-start.6 = ((s8[7372800]{0:T(1024)(128)(4,1)}), s8[4194304]{0:T(1024)(128)(4,1)S(1)}, s32[]{:S(2)}) async-start(s8[7372800]{0:T(1024)(128)(4,1)} %bitcast.333), calls=%async_computation.12 | async-start | bytes 8388608
  877.2 141.1 %slice-start.3 = ((s8[7372800]{0:T(1024)(128)(4,1)}), s8[3178496]{0:T(1024)(128)(4,1)S(1)}, s32[]{:S(2)}) async-start(s8[7372800]{0:T(1024)(128)(4,1)} %bitcast.329), calls=%async_computation.9 | async-start | bytes 6356992
  877.2 141.1 %slice-start.7 = ((s8[7372800]{0:T(1024)(128)(4,1)}), s8[3178496]{0:T(1024)(128)(4,1)S(1)}, s32[]{:S(2)}) async-start(s8[7372800]{0:T(1024)(128)(4,1)} %bitcast.333), calls=%async_computation.13 | async-start | bytes 6356992
  947.7 70.7 %copy-start.5 = (f32[30,30]{1,0:T(8,128)S(1)}, f32[30,30]{1,0:T(8,128)}, u32[]{:S(2)}) copy-start(f32[30,30]{1,0:T(8,128)} %copy-done.4) | copy-start | bytes 10804
  1018.3 15.2 %copy-start.7 = (f32[2048]{0:T(1024)S(1)}, f32[2048]{0:T(1024)}, u32[]{:S(2)}) copy-start(f32[2048]{0:T(1024)} %copy-done.6) | copy-start | bytes 24580
  1018.4 15.1 %copy-start.9 = (f32[2048]{0:T(1024)S(1)}, f32[2048]{0:T(1024)}, u32[]{:S(2)}) copy-start(f32[2048]{0:T(1024)} %copy-done.8) | copy-start | bytes 24580
  1018.4 15.1 %copy-start.11 = (f32[2048]{0:T(1024)S(1)}, f32[2048]{0:T(1024)}, u32[]{:S(2)}) copy-start(f32[2048]{0:T(1024)} %copy-done.10) | copy-start | bytes 24580
  1018.4 15.1 %copy-start.17 = (f32[30]{0:T(128)S(1)}, f32[30]{0:T(128)}, u32[]{:S(2)}) copy-start(f32[30]{0:T(128)} %copy-done.16) | copy-start | bytes 364
  1018.4 15.1 %copy-start.19 = (f32[30]{0:T(128)S(1)}, f32[30]{0:T(128)}, u32[]{:S(2)}) copy-start(f32[30]{0:T(128)} %copy-done.18) | copy-start | bytes 364
  1018.4 15.1 %copy-start.21 = (f32[30]{0:T(128)S(1)}, f32[30]{0:T(128)}, u32[]{:S(2)}) copy-start(f32[30]{0:T(128)} %copy-done.20) | copy-start | bytes 364
  1188.8 75.0 %copy-start.13 = (f32[2048]{0:T(1024)S(1)}, f32[2048]{0:T(1024)}, u32[]{:S(2)}) copy-start(f32[2048]{0:T(1024)} %get-tuple-element.49) | copy-start | bytes 24580
  1188.9 75.0 %copy-start.15 = (f32[2048]{0:T(1024)S(1)}, f32[2048]{0:T(1024)}, u32[]{:S(2)}) copy-start(f32[2048]{0:T(1024)} %get-tuple-element.50) | copy-start | bytes 24580
  1338.6 29.0 %copy-start.23 = (f32[30]{0:T(128)S(1)}, f32[30]{0:T(128)}, u32[]{:S(2)}) copy-start(f32[30]{0:T(128)} %param.7) | copy-start | bytes 364
where the time goes:
time: 1400 us; the launch traced here: 1390 us
  matrix products  1180 us (84%)
  blocking collectives  74.2 us (5%)
  local copies, waits for them, and re-layouts  58.3 us (4%)
  other arithmetic  57.4 us (4%)
  waiting for transfers between devices  14.9 us (1%)
    dot_general x8, matrix products, transform(): jnp.matmul(imag_part, sine, precision=HIGHEST)  297 us
    dot_general x8, matrix products, transform(): jnp.matmul(real_part, sine, precision=HIGHEST)  295 us
    dot_general x8, matrix products, transform(): jnp.matmul(imag_part, cosine, precision=HIGHEST)  294 us
    dot_general x8, matrix products, transform(): jnp.matmul(real_part, cosine, precision=HIGHEST)  292 us
    all_to_all x2, blocking collectives, per_device(): lax.all_to_all(moved, 'freq', split_axis=4, concat_axis=4, tiled=True)  38.8 us
  transfers between devices with their start and end apart: 2, of which 1 were waited for; matrix products, arithmetic and copies ran while one was open for 2% of the time, Pallas kernels for 0%

commit v1 on v0

--- a/solution.py
+++ b/solution.py
@@ -5,6 +5,15 @@
 
 STEPS = 2
 HIGHEST = lax.Precision.HIGHEST
+
+
+def feed_the_stages_all(x_local, bus_axis):
+    return jnp.concatenate(
+        lax.all_to_all(
+            jnp.stack(jnp.split(x_local, lax.axis_size(bus_axis), 4), 0), bus_axis, 0, 0
+        ),
+        4,
+    )
 
 
 def angle_table(first, second, modulus, orient):
@@ -100,11 +109,7 @@
         real_part, imag_part = rotate(inverted[:, 0], inverted[:, 1], untwist_cos, untwist_sin)
         moved = jnp.stack((real_part, imag_part), axis=1).reshape(evolve_rows.shape)
         columns = nonlinear_phase(
-            transform(
-                lax.all_to_all(moved, "freq", split_axis=4, concat_axis=4, tiled=True),
-                inverse_short_cos,
-                inverse_short_sin,
-            )
+            transform(feed_the_stages_all(moved, "freq"), inverse_short_cos, inverse_short_sin)
             * (1.0 / total_count),
             kerr_gain,
         )

time: 1400 us -> 1620 us (1.16)
  local copies, waits for them, and re-layouts: 58.3 us -> 276 us
    split x0 -> x62, local copies, waits for them, and re-layouts: none -> 197 us  [feed_the_stages_all(): jnp.split(x_local, lax.axis_size(bus_axis), 4)]
    unnamed x78 -> x142, local copies, waits for them, and re-layouts: 11.8 us -> 35.5 us
  transfers between devices with their start and end apart: 2 -> 2, of which waited for: 1 -> 1; matrix products, arithmetic and copies ran while one was open for 2% -> 1% of each run, Pallas kernels for 0% -> 0%
where the time goes in v1:
time: 1620 us; the launch traced here: 1610 us
  matrix products  1180 us (73%)
  local copies, waits for them, and re-layouts  276 us (17%)
  blocking collectives  74.6 us (5%)
  other arithmetic  54.6 us (3%)
    dot_general x8, matrix products, transform(): jnp.matmul(imag_part, sine, precision=HIGHEST)  296 us
    dot_general x8, matrix products, transform(): jnp.matmul(real_part, sine, precision=HIGHEST)  295 us
    dot_general x8, matrix products, transform(): jnp.matmul(imag_part, cosine, precision=HIGHEST)  294 us
    dot_general x8, matrix products, transform(): jnp.matmul(real_part, cosine, precision=HIGHEST)  292 us
    split x62, local copies, waits for them, and re-layouts, feed_the_stages_all(): jnp.split(x_local, lax.axis_size(bus_axis), 4)  197 us
    all_to_all x2, blocking collectives, feed_the_stages_all(): lax.all_to_all(jnp.stack(jnp.split(x_local, lax.axis_size(bus_axis), 4),...  39.1 us
    unnamed x142, local copies, waits for them, and re-layouts  35.5 us
  transfers between devices with their start and end apart: 2, of which 1 were waited for; matrix products, arithmetic and copies ran while one was open for 1% of the time, Pallas kernels for 0%

profile of v1, /device:TPU:0, one launch (start us, length us, event | category | flops | bytes accessed | tf_op | source)
XLA Modules:
  0.0 1610.0 jit_solution(1117517528023880022)
XLA Ops:
  4.6 7.3 all-to-all-start
  12.1 14.9 all-to-all-done
  36.1 3.1 all-to-all-start.1
  39.2 19.7 %fusion.352 = (f32[1,30,30,2048]{3,0,2,1:T(1,128)}, f32[1,30,30,2048]{3,0,2,1:T(1,128)}) fusion(f32[2,30,30,2048]{3,0,2,1:T(2,128)} %param.5), kind=kLoop, calls=%fused_computation.446 | loop fusion | bytes 29491200 | tf_op jit(solution)/shard_map/slice | solution.py:79
  65.2 71.2 %fusion.12 = f32[30,2048]{1,0:T(8,128)S(1)} fusion(f32[1,1,30,2048]{3,1,2,0:T(1,128)S(1)} %get-tuple-element.107), kind=kOutput, calls=%fused_computation.15 | convolution fusion | flops 1572864000 | bytes 491520 | tf_op jit(solution)/shard_map/dot_general | solution.py:32
  136.4 71.4 %fusion.10 = f32[30,2048]{1,0:T(8,128)S(1)} fusion(f32[1,1,30,2048]{3,1,2,0:T(1,128)S(1)} %get-tuple-element.108), kind=kOutput, calls=%fused_computation.13 | convolution fusion | flops 1572864000 | bytes 491520 | tf_op jit(solution)/shard_map/dot_general | solution.py:35
  207.8 70.6 %fusion.65 = f32[2048,30]{0,1:T(8,128)S(1)} fusion(f32[30,2048]{1,0:T(8,128)S(1)} %fusion.12, f32[1,1,30,2048]{3,1,2,0:T(1,128)S(1)} %get-tuple-element.108), kind=kOutput, calls=%fused_computation.52 | convolution fusion | flops 1568731136 | bytes 737280 | tf_op jit(solution)/shard_map/dot_general | solution.py:32
  278.4 70.4 %fusion.71 = f32[2048,30]{0,1:T(8,128)S(1)} fusion(f32[30,2048]{1,0:T(8,128)S(1)} %fusion.10, f32[1,1,30,2048]{3,1,2,0:T(1,128)S(1)} %get-tuple-element.107), kind=kOutput, calls=%fused_computation.54 | convolution fusion | flops 1568731136 | bytes 737280 | tf_op jit(solution)/shard_map/dot_general | solution.py:35
  348.9 11.7 multiply_reduce_fusion.6
  364.0 6.9 fusion.100
  370.9 74.2 %fusion.30 = f32[30,2048]{1,0:T(8,128)S(1)} fusion(f32[30,2048]{0,1:T(8,128)S(1)} %get-tuple-element.27), kind=kOutput, calls=%fused_computation.28 | convolution fusion | flops 1568669696 | bytes 491520 | tf_op jit(solution)/shard_map/dot_general | solution.py:32
  445.1 74.4 %fusion.28 = f32[30,2048]{1,0:T(8,128)S(1)} fusion(f32[1,30,2048]{1,2,0:T(8,128)S(1)} %get-tuple-element.28), kind=kOutput, calls=%fused_computation.27 | convolution fusion | flops 1568669696 | bytes 491520 | tf_op jit(solution)/shard_map/dot_general | solution.py:35
  519.6 74.7 %fusion.50 = f32[30,2048]{1,0:T(8,128)S(1)} fusion(f32[30,2048]{1,0:T(8,128)S(1)} %fusion.30, f32[1,30,2048]{1,2,0:T(8,128)S(1)} %get-tuple-element.28), kind=kOutput, calls=%fused_computation.47 | convolution fusion | flops 1568731136 | bytes 737280 | tf_op jit(solution)/shard_map/dot_general | solution.py:32
  594.4 75.0 %multiply_add_fusion.4 = (f32[30,2048]{1,0:T(8,128)S(1)}, f32[30,2048]{1,0:T(8,128)S(1)}) fusion(f32[30,2048]{1,0:T(8,128)S(1)} %fusion.50, f32[2048]{0:T(1024)S(1)} %copy-done.14, f32[2048]{0:T(1024)S(1)} %copy-done.12, f32[30,2048]{1,0:T(8,128)S(1)} %fusion.28, f32[30,2048]{0,1:T(8,128)S(1)} %get-tuple-element.27), kind=kOutput, calls=%fused_computation.157 | convolution fusion | flops 1569099776 | bytes 1245184 | tf_op jit(solution)/shard_map/dot_general | solution.py:35
  670.2 11.4 fusion.356
  681.5 15.4 fusion.355
  703.6 2.8 copy.3272
  711.9 2.8 copy.3269
  714.7 2.8 copy.3268
  717.5 2.8 copy.3267
  745.2 2.8 copy.3283
  759.2 2.8 copy.3278
  762.0 2.8 copy.3277
  764.8 2.8 copy.3276
  783.0 21.2 %all_to_all.30 = f32[32,1,3840]{2,1,0:T(1,128)S(1)} all-to-all(f32[32,1,3840]{2,1,0:T(1,128)S(1)} %reshape.919), channel_id=1, replica_groups=mesh['freq'=32] {'freq'}, dimensions={0} | all-to-all | bytes 983040 | tf_op jit(solution)/shard_map/all_to_all | solution.py:12
  820.1 17.9 %all_to_all.31 = f32[32,1,3840]{2,1,0:T(1,128)S(1)} all-to-all(f32[32,1,3840]{2,1,0:T(1,128)S(1)} %reshape.921), channel_id=1, replica_groups=mesh['freq'=32] {'freq'}, dimensions={0} | all-to-all | bytes 983040 | tf_op jit(solution)/shard_map/all_to_all | solution.py:88
  842.7 71.2 %fusion.8 = f32[30,2048]{1,0:T(8,128)S(1)} fusion(f32[1,1,30,2048]{3,1,2,0:T(1,128)S(1)} %get-tuple-element.105), kind=kOutput, calls=%fused_computation.11 | convolution fusion | flops 1572864000 | bytes 491520 | tf_op jit(solution)/shard_map/dot_general | solution.py:32
  913.9 71.4 %fusion.6 = f32[30,2048]{1,0:T(8,128)S(1)} fusion(f32[1,1,30,2048]{3,1,2,0:T(1,128)S(1)} %get-tuple-element.106), kind=kOutput, calls=%fused_computation.9 | convolution fusion | flops 1572864000 | bytes 491520 | tf_op jit(solution)/shard_map/dot_general | solution.py:35
  985.3 70.6 %fusion.77 = f32[2048,30]{0,1:T(8,128)S(1)} fusion(f32[30,2048]{1,0:T(8,128)S(1)} %fusion.8, f32[1,1,30,2048]{3,1,2,0:T(1,128)S(1)} %get-tuple-element.106), kind=kOutput, calls=%fused_computation.56 | convolution fusion | flops 1568731136 | bytes 737280 | tf_op jit(solution)/shard_map/dot_general | solution.py:32
  1056.0 70.4 %fusion.83 = f32[2048,30]{0,1:T(8,128)S(1)} fusion(f32[30,2048]{1,0:T(8,128)S(1)} %fusion.6, f32[1,1,30,2048]{3,1,2,0:T(1,128)S(1)} %get-tuple-element.105), kind=kOutput, calls=%fused_computation.58 | convolution fusion | flops 1568731136 | bytes 737280 | tf_op jit(solution)/shard_map/dot_general | solution.py:35
  1126.5 11.7 multiply_reduce_fusion.2
  1141.6 6.9 fusion.95
  1148.5 74.2 %fusion.22 = f32[30,2048]{1,0:T(8,128)S(1)} fusion(f32[30,2048]{0,1:T(8,128)S(1)} %get-tuple-element.25), kind=kOutput, calls=%fused_computation.24 | convolution fusion | flops 1568669696 | bytes 491520 | tf_op jit(solution)/shard_map/dot_general | solution.py:32
  1222.7 74.4 %fusion.20 = f32[30,2048]{1,0:T(8,128)S(1)} fusion(f32[1,30,2048]{1,2,0:T(8,128)S(1)} %get-tuple-element.26), kind=kOutput, calls=%fused_computation.23 | convolution fusion | flops 1568669696 | bytes 491520 | tf_op jit(solution)/shard_map/dot_general | solution.py:35
  1297.2 74.7 %fusion.56 = f32[30,2048]{1,0:T(8,128)S(1)} fusion(f32[30,2048]{1,0:T(8,128)S(1)} %fusion.22, f32[1,30,2048]{1,2,0:T(8,128)S(1)} %get-tuple-element.26), kind=kOutput, calls=%fused_computation.49 | convolution fusion | flops 1568731136 | bytes 737280 | tf_op jit(solution)/shard_map/dot_general | solution.py:32
  1371.9 75.0 %multiply_add_fusion.3 = (f32[30,2048]{1,0:T(8,128)S(1)}, f32[30,2048]{1,0:T(8,128)S(1)}) fusion(f32[30,2048]{1,0:T(8,128)S(1)} %fusion.56, f32[2048]{0:T(1024)S(1)} %copy-done.15, f32[2048]{0:T(1024)S(1)} %copy-done.13, f32[30,2048]{1,0:T(8,128)S(1)} %fusion.20, f32[30,2048]{0,1:T(8,128)S(1)} %get-tuple-element.25), kind=kOutput, calls=%fused_computation.155 | convolution fusion | flops 1569099776 | bytes 1245184 | tf_op jit(solution)/shard_map/dot_general | solution.py:35
  1447.8 11.3 fusion.354
  1459.1 15.6 fusion.353
  1483.5 2.8 copy.3333
  1486.4 2.8 copy.3332
  1494.7 2.8 copy.3329
  1522.4 2.8 copy.3345
  1528.0 2.8 copy.3343
  1530.8 2.8 copy.3342
  1533.6 2.8 copy.3341
  1536.4 2.8 copy.3340
  1559.4 17.9 %all_to_all.32 = f32[32,1,3840]{2,1,0:T(1,128)S(1)} all-to-all(f32[32,1,3840]{2,1,0:T(1,128)S(1)} %reshape.923), channel_id=1, replica_groups=mesh['freq'=32] {'freq'}, dimensions={0} | all-to-all | bytes 983040 | tf_op jit(solution)/shard_map/all_to_all | solution.py:12
  1586.9 17.7 %all_to_all.33 = f32[32,1,3840]{2,1,0:T(1,128)S(1)} all-to-all(f32[32,1,3840]{2,1,0:T(1,128)S(1)} %reshape.925), channel_id=1, replica_groups=mesh['freq'=32] {'freq'}, dimensions={0} | all-to-all | bytes 983040 | tf_op jit(solution)/shard_map/all_to_all | solution.py:116
  (266 shorter events, 189.0 us)
Async XLA Ops:
  4.6 22.4 %all-to-all-start = ((f32[32,1,3840]{2,1,0:T(1,128)}), f32[32,1,3840]{2,1,0:T(1,128)S(1)}, u32[]{:S(2)}, u32[]{:S(2)}) async-start(f32[32,1,3840]{2,1,0:T(1,128)} %reshape.915), calls=%async_computation | async-start | bytes 983040 | tf_op jit(solution)/shard_map/all_to_all | solution.py:82
  12.1 46.9 %copy-start = (f32[64,32]{0,1:T(8,128)}, f32[64,32]{0,1:T(8,128)S(1)}, u32[]{:S(2)}) copy-start(f32[64,32]{0,1:T(8,128)S(1)} %get-tuple-element.112) | copy-start | bytes 24580
  12.1 46.9 %copy-start.2 = (f32[64,32]{0,1:T(8,128)}, f32[64,32]{0,1:T(8,128)S(1)}, u32[]{:S(2)}) copy-start(f32[64,32]{0,1:T(8,128)S(1)} %get-tuple-element.113) | copy-start | bytes 24580
  36.1 24.2 %all-to-all-start.1 = ((f32[32,1,3840]{2,1,0:T(1,128)}), f32[32,1,3840]{2,1,0:T(1,128)S(1)}, u32[]{:S(2)}, u32[]{:S(2)}) async-start(f32[32,1,3840]{2,1,0:T(1,128)} %reshape.917), calls=%async_computation.1 | async-start | bytes 983040 | tf_op jit(solution)/shard_map/all_to_all | solution.py:88
  39.2 21.1 %copy-start.24 = (f32[3,30]{1,0:T(4,128)S(1)}, f32[3,30]{1,0:T(4,128)}, u32[]{:S(2)}) copy-start(f32[3,30]{1,0:T(4,128)} %param.6) | copy-start | bytes 1084
  59.0 305.0 %copy-start.6 = (f32[2048]{0:T(1024)}, f32[2048]{0:T(1024)S(1)}, u32[]{:S(2)}) copy-start(f32[2048]{0:T(1024)S(1)} %fusion.210) | copy-start | bytes 24580
  59.0 289.8 %copy-start.4 = (f32[30,30]{1,0:T(8,128)}, f32[30,30]{1,0:T(8,128)S(1)}, u32[]{:S(2)}) copy-start(f32[30,30]{1,0:T(8,128)S(1)} %fusion.171) | copy-start | bytes 10804
  59.7 304.3 %copy-start.8 = (f32[2048]{0:T(1024)}, f32[2048]{0:T(1024)S(1)}, u32[]{:S(2)}) copy-start(f32[2048]{0:T(1024)S(1)} %get-tuple-element.117) | copy-start | bytes 24580
  60.3 303.6 %copy-start.10 = (f32[2048]{0:T(1024)}, f32[2048]{0:T(1024)S(1)}, u32[]{:S(2)}) copy-start(f32[2048]{0:T(1024)S(1)} %get-tuple-element.114) | copy-start | bytes 24580
  60.3 303.6 %copy-start.16 = (f32[30]{0:T(128)}, f32[30]{0:T(128)S(1)}, u32[]{:S(2)}) copy-start(f32[30]{0:T(128)S(1)} %get-tuple-element.109) | copy-start | bytes 364
  60.4 303.6 %copy-start.18 = (f32[30]{0:T(128)}, f32[30]{0:T(128)S(1)}, u32[]{:S(2)}) copy-start(f32[30]{0:T(128)S(1)} %get-tuple-element.110) | copy-start | bytes 364
  60.4 303.6 %copy-start.20 = (f32[30]{0:T(128)}, f32[30]{0:T(128)S(1)}, u32[]{:S(2)}) copy-start(f32[30]{0:T(128)S(1)} %get-tuple-element.111) | copy-start | bytes 364
  207.8 141.0 %slice-start = ((s8[7372800]{0:T(1024)(128)(4,1)}), s8[4194304]{0:T(1024)(128)(4,1)S(1)}, s32[]{:S(2)}) async-start(s8[7372800]{0:T(1024)(128)(4,1)} %bitcast.415), calls=%async_computation.6 | async-start | bytes 8388608
  207.8 141.0 %slice-start.4 = ((s8[7372800]{0:T(1024)(128)(4,1)}), s8[4194304]{0:T(1024)(128)(4,1)S(1)}, s32[]{:S(2)}) async-start(s8[7372800]{0:T(1024)(128)(4,1)} %bitcast.419), calls=%async_computation.10 | async-start | bytes 8388608
  278.4 70.4 %slice-start.1 = ((s8[7372800]{0:T(1024)(128)(4,1)}), s8[3178496]{0:T(1024)(128)(4,1)S(1)}, s32[]{:S(2)}) async-start(s8[7372800]{0:T(1024)(128)(4,1)} %bitcast.415), calls=%async_computation.7 | async-start | bytes 6356992
  278.4 70.4 %slice-start.5 = ((s8[7372800]{0:T(1024)(128)(4,1)}), s8[3178496]{0:T(1024)(128)(4,1)S(1)}, s32[]{:S(2)}) async-start(s8[7372800]{0:T(1024)(128)(4,1)} %bitcast.419), calls=%async_computation.11 | async-start | bytes 6356992
  519.6 74.8 %copy-start.12 = (f32[2048]{0:T(1024)S(1)}, f32[2048]{0:T(1024)}, u32[]{:S(2)}) copy-start(f32[2048]{0:T(1024)} %get-tuple-element.116) | copy-start | bytes 24580
  519.6 74.8 %copy-start.14 = (f32[2048]{0:T(1024)S(1)}, f32[2048]{0:T(1024)}, u32[]{:S(2)}) copy-start(f32[2048]{0:T(1024)} %get-tuple-element.115) | copy-start | bytes 24580
  759.2 50.4 %copy-start.22 = (f32[30]{0:T(128)S(1)}, f32[30]{0:T(128)}, u32[]{:S(2)}) copy-start(f32[30]{0:T(128)} %param.7) | copy-start | bytes 364
  764.8 50.7 %copy-start.1 = (f32[64,32]{0,1:T(8,128)S(1)}, f32[64,32]{0,1:T(8,128)}, u32[]{:S(2)}) copy-start(f32[64,32]{0,1:T(8,128)} %copy-done) | copy-start | bytes 24580
  764.8 50.7 %copy-start.3 = (f32[64,32]{0,1:T(8,128)S(1)}, f32[64,32]{0,1:T(8,128)}, u32[]{:S(2)}) copy-start(f32[64,32]{0,1:T(8,128)} %copy-done.2) | copy-start | bytes 24580
  985.3 141.0 %slice-start.2 = ((s8[7372800]{0:T(1024)(128)(4,1)}), s8[4194304]{0:T(1024)(128)(4,1)S(1)}, s32[]{:S(2)}) async-start(s8[7372800]{0:T(1024)(128)(4,1)} %bitcast.417), calls=%async_computation.8 | async-start | bytes 8388608
  985.3 141.0 %slice-start.6 = ((s8[7372800]{0:T(1024)(128)(4,1)}), s8[4194304]{0:T(1024)(128)(4,1)S(1)}, s32[]{:S(2)}) async-start(s8[7372800]{0:T(1024)(128)(4,1)} %bitcast.421), calls=%async_computation.12 | async-start | bytes 8388608
  1055.9 70.4 %slice-start.3 = ((s8[7372800]{0:T(1024)(128)(4,1)}), s8[3178496]{0:T(1024)(128)(4,1)S(1)}, s32[]{:S(2)}) async-start(s8[7372800]{0:T(1024)(128)(4,1)} %bitcast.417), calls=%async_computation.9 | async-start | bytes 6356992
  1056.0 70.4 %slice-start.7 = ((s8[7372800]{0:T(1024)(128)(4,1)}), s8[3178496]{0:T(1024)(128)(4,1)S(1)}, s32[]{:S(2)}) async-start(s8[7372800]{0:T(1024)(128)(4,1)} %bitcast.421), calls=%async_computation.13 | async-start | bytes 6356992
  1056.0 70.4 %copy-start.5 = (f32[30,30]{1,0:T(8,128)S(1)}, f32[30,30]{1,0:T(8,128)}, u32[]{:S(2)}) copy-start(f32[30,30]{1,0:T(8,128)} %copy-done.4) | copy-start | bytes 10804
  1126.4 15.2 copy-start.7
  1126.4 15.2 copy-start.9
  1126.4 15.2 copy-start.11
  1126.4 15.1 copy-start.17
  1126.4 15.1 copy-start.19
  1126.5 15.1 copy-start.21
  1297.2 74.8 %copy-start.13 = (f32[2048]{0:T(1024)S(1)}, f32[2048]{0:T(1024)}, u32[]{:S(2)}) copy-start(f32[2048]{0:T(1024)} %get-tuple-element.116) | copy-start | bytes 24580
  1297.2 74.8 %copy-start.15 = (f32[2048]{0:T(1024)S(1)}, f32[2048]{0:T(1024)}, u32[]{:S(2)}) copy-start(f32[2048]{0:T(1024)} %get-tuple-element.115) | copy-start | bytes 24580
  1536.4 46.4 %copy-start.23 = (f32[30]{0:T(128)S(1)}, f32[30]{0:T(128)}, u32[]{:S(2)}) copy-start(f32[30]{0:T(128)} %param.7) | copy-start | bytes 364
